TPU v7x, 256 devices: a whole 4x4x8 slice. The times are simulated.
256 devices in a mesh: row: 128 (over z, y, x), width: 2 (over core).
Axes of the slice: x: 4, y: 4, z: 8, core: 2. Of those that a mesh axis runs over, the one named last changes fastest.
Arguments:
- row_numbers: int32 [4096, 2], P('row'), may hold values from 0 to 131071
- item_table: bfloat16 [131072, 64], P('row', 'width'), may hold values from -6 to 6
- dense_part: float32 [4096, 64], P('row', 'width'), may hold values from -6 to 6
- small_ids: int32 [4096], P('row'), may hold values from 0 to 255
- small_table: bfloat16 [256, 64], P('row', 'width'), may hold values from -6 to 6
Outputs:
- features: bfloat16 [4096, 3, 64], P('row', None, 'width')
All inputs are finite; a program needn't handle non-finite values.
Results may differ from a plain program's by a relative error of at most 0.0004.
Values may be sent and summed in bfloat16 or wider, within the bound.
A program may use at most 64 MiB of HBM per device.

v0:
```python
import functools

import jax
import jax.numpy as jnp
from jax import lax
from jax.experimental import pallas as pl
from jax.experimental.pallas import tpu as pltpu
from jax.sharding import PartitionSpec as P

MESH = pl.DeviceIdType.MESH


def near_size(count):
    return max(d for d in range(1, count + 1) if count % d == 0 and d * d <= count)


def target(place, step, count):
    return place ^ step if count & (count - 1) == 0 else (place + step) % count


def source(place, step, count):
    return place ^ step if count & (count - 1) == 0 else (place - step + count) % count


def kernel(
    near, far, scale,
    ids_hbm, table_hbm, dense_hbm, small_ids_hbm, small_hbm, out_ref,
    ids, tables, dense, small_ids, smalls, packed, arrived,
    hits_ref, local_sem, ids_out, ids_in, tab_out, tab_in, sm_out, sm_in, sf_out, sf_in, val_out, val_in,
):
    me = lax.axis_index("row")
    low, high = me % near, me // near
    picks, examples = ids.shape[1:]
    features, rows = tables.shape[1:]
    small_span = smalls.shape[2]

    def near_to(step):
        return {"row": high * near + target(low, step, near)}

    def far_to(step):
        return {"row": target(high, step, far) * near + low}

    def far_back(step):
        return {"row": source(high, step, far) * near + low}

    barrier = pltpu.get_barrier_semaphore()
    for step in range(1, far):
        pl.semaphore_signal(barrier, inc=1, device_id=far_to(step), device_id_type=MESH)
    for step in range(1, near):
        pl.semaphore_signal(barrier, inc=1, device_id=near_to(step), device_id_type=MESH)

    own = [
        pltpu.make_async_copy(src, dst, local_sem.at[i])
        for i, (src, dst) in enumerate(
            [
                (ids_hbm, ids.at[0]),
                (table_hbm, tables.at[0]),
                (small_hbm, smalls.at[0, 0]),
                (dense_hbm, dense),
                (small_ids_hbm, small_ids),
            ]
        )
    ]
    for copy in own:
        copy.start()

    def remote(src, dst, out_sem, in_sem, device):
        return pltpu.make_async_remote_copy(
            src_ref=src, dst_ref=dst, send_sem=out_sem, recv_sem=in_sem,
            device_id=device, device_id_type=MESH,
        )

    ids_copies = [
        remote(ids.at[0], ids.at[s], ids_out.at[s], ids_in.at[s], far_to(s)) for s in range(1, far)
    ]
    table_copies = [
        remote(tables.at[0], tables.at[s], tab_out.at[s], tab_in.at[s], near_to(s))
        for s in range(1, near)
    ]
    small_copies = [
        remote(smalls.at[0, 0], smalls.at[0, s], sm_out.at[s], sm_in.at[s], near_to(s))
        for s in range(1, near)
    ]
    small_far = [
        remote(smalls.at[0], smalls.at[s], sf_out.at[s], sf_in.at[s], far_to(s))
        for s in range(1, far)
    ]
    value_copies = [
        remote(packed.at[s], arrived.at[s], val_out.at[s], val_in.at[s], far_back(s))
        for s in range(1, far)
    ]

    own[0].wait()
    pl.semaphore_wait(barrier, far - 1 + near - 1)
    for copy in reversed(ids_copies):
        copy.start()
    own[2].wait()
    for copy in small_copies:
        copy.start()
    own[1].wait()
    for copy in reversed(table_copies):
        copy.start()

    own[3].wait()
    own[4].wait()
    out_ref[0] = dense[...].astype(out_ref.dtype)

    for copy in ids_copies:
        copy.wait_recv()
    wanted = jnp.concatenate([ids[s] for s in range(far)], axis=1)
    lanes = far * examples
    spot = lax.broadcasted_iota(jnp.int32, (rows, lanes), 0)

    def chosen(step):
        first = (high * near + source(low, step, near)) * rows
        hits = 0.0
        for pick in range(picks):
            hits = hits + jnp.where(spot == wanted[pick : pick + 1] - first, 1.0, 0.0)
        return hits.astype(tables.dtype)

    for step in range(near):
        hits_ref[step] = chosen(step)
    for copy in small_copies:
        copy.wait_recv()
    for copy in reversed(small_far):
        copy.start()
    found = jnp.zeros((features, lanes), jnp.float32)
    for step in [0, *reversed(range(1, near))]:
        if step:
            table_copies[step - 1].wait_recv()
        found = found + jnp.dot(tables[step], hits_ref[step], preferred_element_type=jnp.float32)

    blocks = features // 8
    for step in reversed(range(far)):
        packed[step] = jnp.concatenate(
            [
                found[8 * b : 8 * b + 8, step * examples : (step + 1) * examples]
                for b in range(blocks)
            ],
            axis=1,
        )
        if step:
            value_copies[step - 1].start()

    small_column = jnp.broadcast_to(small_ids[...], (8, examples)).T[:, 0:1]
    for copy in small_far:
        copy.wait_recv()
    rows_out = jnp.zeros((examples, features), jnp.float32)
    for far_step in range(far):
        for near_step in range(near):
            device = source(high, far_step, far) * near + source(low, near_step, near)
            part = smalls[far_step, near_step].astype(jnp.float32)
            for r in range(small_span):
                rows_out = jnp.where(
                    small_column == device * small_span + r, part[r : r + 1], rows_out
                )
    out_ref[2] = rows_out.astype(out_ref.dtype)

    total = packed[0]
    for step in range(1, far):
        value_copies[step - 1].wait_recv()
        total = total + arrived[step]
    total = total * scale
    pooled = jnp.concatenate(
        [total[:, b * examples : (b + 1) * examples] for b in range(blocks)], axis=0
    ).T
    out_ref[1] = pooled.astype(out_ref.dtype)

    for copy in ids_copies + table_copies + small_copies + small_far + value_copies:
        copy.wait_send()


def per_device(count, row_numbers, item_table, dense_part, small_ids, small_table):
    near = near_size(count)
    far = count // near
    examples, picks = row_numbers.shape
    rows, features = item_table.shape
    dma = pltpu.SemaphoreType.DMA
    out = pl.pallas_call(
        functools.partial(kernel, near, far, picks ** (-0.5)),
        out_shape=pltpu.VMEM((3, examples, features), jnp.bfloat16),
        in_specs=[pl.BlockSpec(memory_space=pl.ANY)] * 5,
        out_specs=pl.BlockSpec(memory_space=pltpu.VMEM),
        scratch_shapes=[
            pltpu.VMEM((far, picks, examples), jnp.int32),
            pltpu.VMEM((near, features, rows), item_table.dtype),
            pltpu.VMEM(dense_part.shape, dense_part.dtype),
            pltpu.VMEM((1, examples), jnp.int32),
            pltpu.VMEM((far, near) + small_table.shape, small_table.dtype),
            pltpu.VMEM((far, 8, features // 8 * examples), jnp.float32),
            pltpu.VMEM((far, 8, features // 8 * examples), jnp.float32),
            pltpu.VMEM((near, rows, far * examples), item_table.dtype),
            dma((5,)),
            dma((far,)), dma((far,)),
            dma((near,)), dma((near,)),
            dma((near,)), dma((near,)),
            dma((far,)), dma((far,)),
            dma((far,)), dma((far,)),
        ],
        compiler_params=pltpu.CompilerParams(collective_id=0, has_side_effects=True),
    )(row_numbers.T, item_table.T, dense_part, small_ids[None, :], small_table)
    return jnp.transpose(out, (1, 0, 2))


def solution(mesh):
    placed = (P("row", None), P("row", "width"), P("row", "width"), P("row"), P("row", "width"))
    return jax.shard_map(
        functools.partial(per_device, mesh.shape["row"]),
        mesh=mesh, in_specs=placed, out_specs=P("row", None, "width"), check_vma=False,
    )
```

profile of v0, /device:TPU:4, one launch (start us, length us, event | category | flops | bytes accessed | tf_op | source)
XLA Modules:
  0.0 32.4 jit_solution(1199457991842759469)
XLA Ops:
  0.0 31.8 %shard_map.55 = bf16[3,32,32]{2,1,0:T(8,128)(2,1)S(1)} custom-call(s32[2,32]{1,0:T(2,128)} %bitcast.6, bf16[32,1024]{1,0:T(8,128)(2,1)} %bitcast.5, f32[32,32]{1,0:T(8,128)} %dense_hbm.1, s32[1,32]{1,0:T(1,128)} %bitcast.7, bf16[2,32]{1,0:T(2,128)(2,1)} %small_hbm.1), custom_call_target="tpu_custom_call" | custom-call | tf_op jit(solution)/shard_map/pallas_call | solution.py:179
  31.8 0.6 %copy.7 = bf16[32,3,32]{2,0,1:T(8,128)(2,1)} copy(bf16[32,3,32]{2,0,1:T(8,128)(2,1)S(1)} %bitcast.4) | data formatting | bytes 12288
where the time goes:
time: 32.5 us; the launch traced here: 32.4 us
  Pallas kernels  31.8 us (98%)
  local copies, waits for them, and re-layouts  0.61 us (2%)
    pallas_call x1, Pallas kernels, per_device(): pl.pallas_call(functools.partial(kernel, near, far, picks ** (-0.5)), out...  31.8 us

commit v1 on v0

v1 whole, which is shorter than its diff:
```python
import functools

import jax
import jax.numpy as jnp
from jax import lax
from jax.experimental import pallas as pl
from jax.experimental.pallas import tpu as pltpu
from jax.sharding import PartitionSpec as P

MESH = pl.DeviceIdType.MESH
LANES = 128
GROUP = 256


def masks(bits):
    out = [0]
    for bit in bits:
        out = out + [m | 1 << bit for m in out]
    return out


def drain(view, sem):
    pltpu.make_async_copy(view, view, sem).wait()


def kernel(
    near_masks, far_masks, scale,
    ids_hbm, table_hbm, dense_hbm, small_ids_hbm, small_hbm, out_ref,
    ids, tables, dense, small_ids, smalls, packed, arrived,
    local_sem, send_sem, ids_sem, table_sem, small_sem, far_sem, value_sem,
):
    me = lax.axis_index("row")
    near, far = len(near_masks), len(far_masks)
    picks, examples = ids.shape[1:]
    features, rows = tables.shape[1:]
    span = smalls.shape[2]
    per_tile = LANES // examples
    tiles = far // per_tile
    chunks = rows // GROUP

    def peer(mask):
        return {"row": me ^ mask}

    barrier = pltpu.get_barrier_semaphore()
    for mask in [*reversed(far_masks[1:]), *reversed(near_masks[1:])]:
        pl.semaphore_signal(barrier, inc=1, device_id=peer(mask), device_id_type=MESH)

    own = [
        pltpu.make_async_copy(src, dst, local_sem.at[i])
        for i, (src, dst) in enumerate(
            [
                (ids_hbm, ids.at[0]),
                (small_hbm, smalls.at[0, 0]),
                (table_hbm, tables.at[0]),
                (dense_hbm, dense),
                (small_ids_hbm, small_ids),
            ]
        )
    ]
    for copy in own:
        copy.start()

    def remote(src, dst, kind, arrival, mask):
        return pltpu.make_async_remote_copy(
            src_ref=src, dst_ref=dst, send_sem=send_sem.at[kind], recv_sem=arrival,
            device_id=peer(mask), device_id_type=MESH,
        )

    with jax.named_scope("barrier"):
        own[0].wait()
        pl.semaphore_wait(barrier, far - 1 + near - 1)
    for s in reversed(range(1, far)):
        remote(ids.at[0], ids.at[s], 0, ids_sem.at[s // per_tile], far_masks[s]).start()
    own[1].wait()
    for s in range(1, near):
        remote(smalls.at[0, 0], smalls.at[0, s], 1, small_sem, near_masks[s]).start()
    own[2].wait()
    for s in reversed(range(1, near)):
        remote(tables.at[0], tables.at[s], 2, table_sem.at[s], near_masks[s]).start()

    own[3].wait()
    own[4].wait()
    out_ref[0] = dense[...].astype(out_ref.dtype)

    with jax.named_scope("smallnear"):
        drain(smalls.at[0, pl.ds(1, near - 1)], small_sem)
    for s in reversed(range(1, far)):
        remote(smalls.at[0], smalls.at[s], 3, far_sem, far_masks[s]).start()

    with jax.named_scope("idswait"):
        drain(ids.at[pl.ds(1, per_tile - 1)], ids_sem.at[0])
        for k in range(1, tiles):
            drain(ids.at[pl.ds(k * per_tile, per_tile)], ids_sem.at[k])
    with jax.named_scope("tabwait"):
        for s in range(1, near):
            drain(tables.at[s], table_sem.at[s])

    near_bits = near_masks[-1]
    spot = lax.broadcasted_iota(jnp.int32, (GROUP, LANES), 0)
    stack = jnp.concatenate(
        [tables[t, :, c * GROUP : (c + 1) * GROUP] for t in range(near) for c in range(chunks)], axis=0
    )
    with jax.named_scope("compute"):
        for k in reversed(range(tiles)):
            wanted = jnp.concatenate(
                [ids[k * per_tile + i] for i in range(per_tile)], axis=1
            )
            low = wanted % GROUP
            chunk = wanted // GROUP % chunks
            owner = (wanted // rows) ^ me
            hits = jnp.concatenate(
                [
                    jnp.where(spot == low[p : p + 1], 1.0, 0.0).astype(tables.dtype)
                    for p in range(picks)
                ],
                axis=1,
            )
            found = jnp.dot(stack, hits, preferred_element_type=jnp.float32)
            total = jnp.zeros((features, LANES), jnp.float32)
            for p in range(picks):
                chosen = jnp.zeros((features, LANES), jnp.float32)
                for t in range(near):
                    for c in range(chunks):
                        j = t * chunks + c
                        want = owner[p : p + 1] * chunks + chunk[p : p + 1]
                        chosen = jnp.where(
                            want == near_masks[t] * chunks + c,
                            found[j * features : (j + 1) * features, p * LANES : (p + 1) * LANES],
                            chosen,
                        )
                total = total + chosen
            for i in reversed(range(per_tile)):
                s = k * per_tile + i
                packed[s] = jnp.concatenate(
                    [
                        total[8 * b : 8 * b + 8, i * examples : (i + 1) * examples]
                        for b in range(features // 8)
                    ],
                    axis=1,
                )
                if s:
                    remote(packed.at[s], arrived.at[s], 4, value_sem, far_masks[s]).start()

    with jax.named_scope("smallwait"):
        drain(smalls.at[pl.ds(1, far - 1)], far_sem)
    with jax.named_scope("rows"):
        column = jnp.broadcast_to(small_ids[...], (8, examples)).T[:, 0:1]
        place = jnp.broadcast_to(column ^ (me * span), (examples, features))
        rows_out = jnp.zeros((examples, features), jnp.float32)
        for f in range(far):
            for n in range(near):
                part = smalls[f, n].astype(jnp.float32)
                for r in range(span):
                    rows_out = jnp.where(
                        place == (far_masks[f] | near_masks[n]) * span + r, part[r : r + 1], rows_out
                    )
        out_ref[2] = rows_out.astype(out_ref.dtype)

    with jax.named_scope("valwait"):
        drain(arrived.at[pl.ds(1, far - 1)], value_sem)
    total = packed[0]
    for s in range(1, far):
        total = total + arrived[s]
    total = total * scale
    pooled = jnp.concatenate(
        [total[:, b * examples : (b + 1) * examples] for b in range(features // 8)], axis=0
    ).T
    out_ref[1] = pooled.astype(out_ref.dtype)

    with jax.named_scope("sendwait"):
        drain(ids.at[pl.ds(1, far - 1)], send_sem.at[0])
        drain(smalls.at[0, pl.ds(1, near - 1)], send_sem.at[1])
        drain(tables.at[pl.ds(1, near - 1)], send_sem.at[2])
        drain(smalls.at[pl.ds(1, far - 1)], send_sem.at[3])
        drain(packed.at[pl.ds(1, far - 1)], send_sem.at[4])


def per_device(near_bits, far_bits, row_numbers, item_table, dense_part, small_ids, small_table):
    near_masks, far_masks = masks(near_bits), masks(far_bits)
    near, far = len(near_masks), len(far_masks)
    examples, picks = row_numbers.shape
    rows, features = item_table.shape
    tiles = far * examples // LANES
    dma = pltpu.SemaphoreType.DMA
    out = pl.pallas_call(
        functools.partial(kernel, near_masks, far_masks, picks ** (-0.5)),
        out_shape=pltpu.VMEM((3, examples, features), jnp.bfloat16),
        in_specs=[pl.BlockSpec(memory_space=pl.ANY)] * 5,
        out_specs=pl.BlockSpec(memory_space=pltpu.VMEM),
        scratch_shapes=[
            pltpu.VMEM((far, picks, examples), jnp.int32),
            pltpu.VMEM((near, features, rows), item_table.dtype),
            pltpu.VMEM(dense_part.shape, dense_part.dtype),
            pltpu.VMEM((1, examples), jnp.int32),
            pltpu.VMEM((far, near) + small_table.shape, small_table.dtype),
            pltpu.VMEM((far, 8, features // 8 * examples), jnp.float32),
            pltpu.VMEM((far, 8, features // 8 * examples), jnp.float32),
            dma((5,)), dma((5,)), dma((tiles,)), dma((near,)), dma, dma, dma,
        ],
        compiler_params=pltpu.CompilerParams(collective_id=0, has_side_effects=True),
    )(row_numbers.T, item_table.T, dense_part, small_ids[None, :], small_table)
    return jnp.transpose(out, (1, 0, 2))


NEAR = (2, 3)
FAR = (0, 1, 4, 5, 6)


def solution(mesh):
    placed = (P("row", None), P("row", "width"), P("row", "width"), P("row"), P("row", "width"))
    return jax.shard_map(
        functools.partial(per_device, NEAR, FAR),
        mesh=mesh, in_specs=placed, out_specs=P("row", None, "width"), check_vma=False,
    )
```

time: 32.5 us -> 24.4 us (0.75)
  the two profiles are of different devices: /device:TPU:4 before, /device:TPU:1 now
where the time goes in v1:
time: 24.4 us; the launch traced here: 24.3 us
  Pallas kernels  23.7 us (97%)
  local copies, waits for them, and re-layouts  0.61 us (2%)
    pallas_call x1, Pallas kernels, per_device(): pl.pallas_call(functools.partial(kernel, near_masks, far_masks, picks **...  23.7 us
    unnamed x1, local copies, waits for them, and re-layouts  0.61 us

profile of v1, /device:TPU:1, one launch (start us, length us, event | category | flops | bytes accessed | tf_op | source)
XLA Modules:
  0.0 24.3 jit_solution(1874762354020304488)
XLA Ops:
  0.0 23.7 %shard_map.55 = bf16[3,32,32]{2,1,0:T(8,128)(2,1)S(1)} custom-call(s32[2,32]{1,0:T(2,128)} %bitcast.6, bf16[32,1024]{1,0:T(8,128)(2,1)} %bitcast.5, f32[32,32]{1,0:T(8,128)} %dense_hbm.1, s32[1,32]{1,0:T(1,128)} %bitcast.7, bf16[2,32]{1,0:T(2,128)(2,1)} %small_hbm.1), custom_call_target="tpu_custom_call" | custom-call | tf_op jit(solution)/shard_map/pallas_call | solution.py:185
  23.7 0.6 %copy.7 = bf16[32,3,32]{2,0,1:T(8,128)(2,1)} copy(bf16[32,3,32]{2,0,1:T(8,128)(2,1)S(1)} %bitcast.4) | data formatting | bytes 12288
